TPU v7x, 64 devices: a 2x2x8 block of a 4x4x8 slice. The times are simulated.
64 devices in a mesh: dp: 4 (over x, y), tp: 16 (over z, core).
Axes of the slice: x: 2, y: 2, z: 8, core: 2. Of those that a mesh axis runs over, the one named last changes fastest.
The devices are a block of a 4x4x8 slice.
Arguments:
- hidden: bfloat16 [16384, 512], P(('dp', 'tp')), parts along dimension 0
- w_two: bfloat16 [512, 512], replicated
- ln_scale: float32 [2, 512], replicated
- ln_shift: float32 [2, 512], replicated
- embed: bfloat16 [51200, 512], P('tp')
- targets: int32 [2, 16384], P(None, ('dp', 'tp')), parts along dimension 1
- loss_mask: int32 [2, 16384], P(None, ('dp', 'tp')), parts along dimension 1
Outputs:
- output 1: float32 [2, 16384], P(None, ('dp', 'tp')), parts along dimension 1
- output 2: float32 [4], P('dp'), parts along dimension 0
- output 3: bfloat16 [16384, 512], P(('dp', 'tp')), parts along dimension 0
- output 4: float32 [204800, 512], P(('dp', 'tp')), parts along dimension 0
- output 5: float32 [2048, 512], P('dp'), parts along dimension 0
- output 6: float32 [8, 512], P('dp'), parts along dimension 0
- output 7: float32 [8, 512], P('dp'), parts along dimension 0
There are 4 independent parts. A program takes and returns all parts, laid end to end along the dimension named above; an argument that names none is the same for every part.
All inputs are finite; a program needn't handle non-finite values.
Results may differ from a plain program's by a relative error of at most 0.001.
Values are sent between devices in bfloat16 or wider.
A program may use at most 768 MiB of HBM per device.

v0:
```python
import jax
import jax.numpy as jnp
from jax import lax
from jax.sharding import PartitionSpec as P

LN_EPS = 1e-5


def layer_norm(values, gain, bias):
    mean_val = jnp.mean(values, axis=-1, keepdims=True)
    centered = values - mean_val
    variance = jnp.mean(centered * centered, axis=-1, keepdims=True)
    return centered * lax.rsqrt(variance + LN_EPS) * gain + bias


def solution(mesh):
    tok_spec = P(('dp', 'tp'), None)
    row_spec = P(None, ('dp', 'tp'))

    def device_step(hidden, w_two, ln_scale, ln_shift, embed, targets, loss_mask):
        tok_rows = hidden.shape[0]
        shard_rows = embed.shape[0]
        shard_idx = lax.axis_index('tp')
        proj_out = jnp.dot(hidden, w_two, preferred_element_type=jnp.float32).astype(jnp.bfloat16)
        norm_input = jnp.stack([hidden.astype(jnp.float32), proj_out.astype(jnp.float32)])
        normed, ln_back = jax.vjp(jax.vmap(layer_norm), norm_input, ln_scale, ln_shift)
        x_loc = normed.astype(jnp.bfloat16)
        x_all = lax.all_gather(x_loc, 'tp', axis=1, tiled=True)
        int_all = lax.all_gather(jnp.stack([targets, loss_mask]), 'tp', axis=2, tiled=True)
        tgt_all = int_all[0]
        mask_all = int_all[1].astype(jnp.float32)
        logits = jnp.einsum('hsd,vd->hsv', x_all, embed, preferred_element_type=jnp.float32)
        local_max = jnp.max(logits, axis=-1)
        exp_loc = jnp.exp(logits - local_max[..., None])
        col_ids = lax.broadcasted_iota(jnp.int32, (1, 1, shard_rows), 2) + shard_idx * shard_rows
        is_target = col_ids == tgt_all[..., None]
        tgt_loc = jnp.sum(jnp.where(is_target, logits, 0.0), axis=-1)
        glob_max = lax.pmax(local_max, 'tp')
        part_stats = jnp.stack([jnp.sum(exp_loc, axis=-1) * jnp.exp(local_max - glob_max), tgt_loc])
        glob_stats = lax.psum(part_stats, 'tp')
        log_norm = glob_max + jnp.log(glob_stats[0])
        token_count = jnp.sum(mask_all, axis=1)
        weight = mask_all / token_count[:, None]
        loss_all = (log_norm - glob_stats[1]) * mask_all
        total_loss = jnp.sum(loss_all / token_count[:, None]).reshape(1)
        token_loss = lax.dynamic_slice_in_dim(loss_all, shard_idx * tok_rows, tok_rows, axis=1)
        softmax_val = exp_loc * jnp.exp(local_max - log_norm)[..., None]
        d_logits = (jnp.where(is_target, softmax_val - 1.0, softmax_val) * weight[..., None]).astype(jnp.bfloat16)
        d_embed = jnp.einsum('hsv,hsd->vd', d_logits, x_all, preferred_element_type=jnp.float32)
        dx_part = jnp.einsum('hsv,vd->hsd', d_logits, embed, preferred_element_type=jnp.float32)
        dx_loc = lax.psum_scatter(dx_part, 'tp', scatter_dimension=1, tiled=True)
        d_norm_in, d_scale_part, d_shift_part = ln_back(dx_loc)
        d_proj = d_norm_in[1].astype(jnp.bfloat16)
        d_hidden = (d_norm_in[0] + jnp.einsum('td,ed->te', d_proj, w_two, preferred_element_type=jnp.float32)).astype(jnp.bfloat16)
        d_w_part = jnp.einsum('te,td->ed', hidden, d_proj, preferred_element_type=jnp.float32)
        d_w_two, d_scale, d_shift = lax.psum((d_w_part, d_scale_part, d_shift_part), 'tp')
        return token_loss, total_loss, d_hidden, d_embed, d_w_two, d_scale, d_shift

    return jax.shard_map(device_step, mesh=mesh,
                         in_specs=(tok_spec, P(), P(), P(), P('tp', None), row_spec, row_spec),
                         out_specs=(row_spec, P('dp'), tok_spec, tok_spec, P('dp', None), P('dp', None), P('dp', None)),
                         check_vma=False)
```

profile of v0, /device:TPU:21, one launch (start us, length us, event | category | flops | bytes accessed | tf_op | source)
XLA Modules:
  0.0 604.3 jit_solution(6403842179392663439)
XLA Ops:
  7.2 0.0 copy-start
  7.2 0.1 all-gather.2.cloned.1.call-start
  7.3 1.6 fusion.15
  8.8 0.0 copy-start.2
  8.8 1.2 convert_reduce_fusion
  10.1 0.0 copy-start.4
  10.1 1.2 fusion.19
  11.3 0.0 copy-start.9
  11.3 0.6 copy-done.9
  11.9 0.0 copy-done.2
  11.9 0.0 copy-done.4
  11.9 0.0 copy-start.7
  11.9 0.6 copy-done.7
  12.5 2.0 fusion.17
  14.5 0.1 all-gather.2.cloned.1.call-update
  14.6 0.1 all-reduce.4.cloned.1.call-start
  14.7 0.7 pad_add_fusion
  15.4 23.0 %all_gather.7 = s32[2,2,4096]{2,1,0:T(2,128)S(1)} all-gather(s32[2,2,256]{2,1,0:T(2,128)S(1)} %pad_add_fusion), channel_id=1, replica_groups=mesh['dp'=4,'tp'=16] {'tp'}, dimensions={2}, use_global_device_ids=true | all-gather | bytes 69632 | tf_op jit(solution)/shard_map/all_gather | solution.py:29
  38.4 34.0 %all-gather.2.cloned.1.call-done = bf16[2,4096,512]{2,1,0:T(8,128)(2,1)} async-done(((bf16[2,256,512]{2,1,0:T(8,128)(2,1)}), bf16[2,4096,512]{2,1,0:T(8,128)(2,1)}) %all-gather.2.cloned.1.call-update) | async-done | bytes 8388624 | tf_op jit(solution)/shard_map/all_gather | solution.py:28
  72.4 0.0 copy-done
  72.4 41.4 %fusion.33 = (f32[2,4096]{1,0:T(2,128)S(1)}, f32[2,4096,3200]{1,2,0:T(8,128)}) fusion(bf16[2,4096,512]{2,1,0:T(8,128)(2,1)} %all-gather.2.cloned.1.call-done, bf16[3200,512]{1,0:T(8,128)(2,1)S(1)} %copy-done), kind=kOutput, calls=%fused_computation.60 | convolution fusion | flops 26869751808 | bytes 116555776 | tf_op jit(solution)/shard_map/hsd,vd->hsv/dot_general | solution.py:32
  113.8 43.6 %pmax.7 = f32[2,4096]{1,0:T(2,128)S(1)} all-reduce(f32[2,4096]{1,0:T(2,128)S(1)} %get-tuple-element.26), channel_id=1, replica_groups=mesh['dp'=4,'tp'=16] {'tp'}, use_global_device_ids=true, to_apply=%region_3.4 | all-reduce | flops 8192 | bytes 65536 | tf_op jit(solution)/shard_map/pmax | solution.py:38
  157.4 32.7 %fusion.3 = (f32[2,4096]{1,0:T(2,128)S(1)}, f32[2,4096]{1,0:T(2,128)S(1)}) fusion(f32[2,4096,3200]{1,2,0:T(8,128)} %get-tuple-element.27, f32[2,4096]{1,0:T(2,128)S(1)} %get-tuple-element.26, s32[2,4096]{1,0:T(2,128)S(1)} %slice_bitcast_fusion.2, s32[3200]{0:T(1024)S(1)} %iota_add_fusion), kind=kLoop, calls=%fused_computation.6 | loop fusion | flops 131055616 | bytes 105001472 | tf_op jit(solution)/shard_map/reduce_sum | solution.py:39
  190.2 0.7 pad_maximum_fusion.1
  190.9 0.1 all-reduce.4.cloned.1.call-update
  191.0 0.2 reduce-scatter.2.cloned.1.call-start
  191.2 0.1 fusion.29
  191.4 103.5 %all-reduce.4.cloned.1.call-done = f32[2,2,4096]{2,1,0:T(2,128)} async-done(((f32[2,2,4096]{2,1,0:T(2,128)}), f32[2,2,4096]{2,1,0:T(2,128)}) %all-reduce.4.cloned.1.call-update) | async-done | bytes 65552 | tf_op jit(solution)/shard_map/psum | solution.py:40
  294.8 2.0 divide_reduce_fusion
  296.9 51.1 %fusion.2 = bf16[2,4096,3200]{1,2,0:T(8,128)(2,1)} fusion(f32[2,4096,3200]{1,2,0:T(8,128)} %get-tuple-element.27, f32[2,4096]{1,0:T(2,128)S(1)} %get-tuple-element.25, f32[2,4096]{1,0:T(2,128)S(1)} %get-tuple-element.24, s32[2,4096]{1,0:T(2,128)S(1)} %slice_bitcast_fusion.2, f32[2,4096]{1,0:T(2,128)S(1)} %get-tuple-element.26, s32[3200]{0:T(1024)S(1)} %iota_add_fusion), kind=kLoop, calls=%fused_computation.4 | loop fusion | flops 183500800 | bytes 157430272 | tf_op jit(solution)/shard_map/convert_element_type | solution.py:48
  348.0 0.0 copy-start.1
  348.0 0.0 copy-start.5
  348.0 0.0 copy-start.6
  348.0 0.0 copy-start.10
  348.0 0.0 copy-start.8
  348.0 36.0 %fusion.4 = f32[2,4096,512]{2,1,0:T(8,128)} fusion(bf16[2,4096,3200]{1,2,0:T(8,128)(2,1)} %fusion.2, bf16[3200,512]{1,0:T(8,128)(2,1)S(1)} %copy-done), kind=kOutput, calls=%fused_computation.8 | convolution fusion | flops 26843545600 | bytes 72482816 | tf_op jit(solution)/shard_map/hsv,vd->hsd/dot_general | solution.py:50
  384.0 0.1 reduce-scatter.2.cloned.1.call-update
  384.0 0.3 all-reduce.6.cloned.1.call-start
  384.3 97.6 %reduce-scatter.2.cloned.1.call-done = f32[2,256,512]{2,1,0:T(8,128)} async-done(((f32[2,4096,512]{2,1,0:T(8,128)}), f32[2,256,512]{2,1,0:T(8,128)}) %reduce-scatter.2.cloned.1.call-update) | async-done | bytes 1048592 | tf_op jit(solution)/shard_map/reduce_scatter | solution.py:51
  481.9 0.0 copy-done.1
  481.9 0.0 copy-done.5
  481.9 0.0 copy-done.6
  481.9 2.2 fusion.31
  484.1 0.0 copy-done.10
  484.1 0.0 copy-done.8
  484.1 1.9 fusion.18
  486.0 1.6 broadcast_add_fusion
  487.7 0.0 copy-start.3
  487.7 1.0 copy-done.3
  488.6 1.4 convolution_bitcast_fusion.1
  490.0 0.1 all-reduce.6.cloned.1.call-update
  490.1 0.0 copy-start.11
  490.1 35.3 %convolution_bitcast_fusion = f32[3200,512]{1,0:T(8,128)} fusion(bf16[2,4096,3200]{1,2,0:T(8,128)(2,1)} %fusion.2, bf16[2,4096,512]{2,1,0:T(8,128)(2,1)} %all-gather.2.cloned.1.call-done), kind=kOutput, calls=%fused_computation.7 | convolution fusion | flops 26843545600 | bytes 67371008 | tf_op jit(solution)/shard_map/hsv,hsd->vd/dot_general | solution.py:49
  525.4 1.2 constant_dynamic-slice_fusion
  526.6 0.0 copy-done.11
  526.6 25.4 %all-reduce = (f32[2,512]{1,0:T(2,128)}, f32[2,512]{1,0:T(2,128)}) all-reduce(f32[2,512]{1,0:T(2,128)S(1)} %get-tuple-element.16, f32[2,512]{1,0:T(2,128)S(1)} %copy-done.11), channel_id=1, replica_groups=mesh['dp'=4,'tp'=16] {'tp'}, use_global_device_ids=true, to_apply=%region_14.15 | all-reduce | flops 2048 | bytes 16384 | tf_op jit(solution)/shard_map/psum | solution.py:56
  551.9 2.4 fusion.12
  554.3 40.9 %all-reduce.6.cloned.1.call-done = f32[512,512]{0,1:T(8,128)} async-done(((f32[512,512]{0,1:T(8,128)}), f32[512,512]{0,1:T(8,128)}) %all-reduce.6.cloned.1.call-update) | async-done | bytes 1048592 | tf_op jit(solution)/shard_map/psum | solution.py:56
  595.3 2.5 copy.15
  (7 shorter events, 0.1 us)
Async XLA Ops:
  7.2 65.2 %copy-start = (bf16[3200,512]{1,0:T(8,128)(2,1)S(1)}, bf16[3200,512]{1,0:T(8,128)(2,1)}, u32[]{:S(2)}) copy-start(bf16[3200,512]{1,0:T(8,128)(2,1)} %param.11) | copy-start | bytes 9830404
  7.2 65.2 %all-gather.2.cloned.1.call-start = ((), (), s32[]{:S(2)}) async-start(), calls=%async_computation.1 | async-start | bytes 8912896 | tf_op jit(solution)/shard_map/all_gather | solution.py:28
  8.8 3.1 copy-start.2
  10.1 1.8 copy-start.4
  11.3 0.6 copy-start.9
  11.9 0.6 copy-start.7
  14.6 280.3 %all-reduce.4.cloned.1.call-start = ((), (), s32[]{:S(2)}) async-start(), calls=%async_computation.2 | async-start | bytes 131072 | tf_op jit(solution)/shard_map/psum | solution.py:40
  191.0 291.0 %reduce-scatter.2.cloned.1.call-start = ((), (), s32[]{:S(2)}) async-start(), calls=%async_computation.3 | async-start | bytes 17825792 | tf_op jit(solution)/shard_map/reduce_scatter | solution.py:51
  348.0 134.0 %copy-start.1 = (bf16[256,512]{1,0:T(8,128)(2,1)S(1)}, bf16[256,512]{1,0:T(8,128)(2,1)}, u32[]{:S(2)}) copy-start(bf16[256,512]{1,0:T(8,128)(2,1)} %param.7) | copy-start | bytes 786436
  348.0 134.0 %copy-start.5 = (f32[2,256]{1,0:T(2,128)S(1)}, f32[2,256]{1,0:T(2,128)}, u32[]{:S(2)}) copy-start(f32[2,256]{1,0:T(2,128)} %copy-done.4) | copy-start | bytes 6148
  348.0 134.0 %copy-start.6 = (f32[2,512]{1,0:T(2,128)S(1)}, f32[2,512]{1,0:T(2,128)}, u32[]{:S(2)}) copy-start(f32[2,512]{1,0:T(2,128)} %param.9) | copy-start | bytes 12292
  348.0 136.1 %copy-start.10 = (f32[2,256]{1,0:T(2,128)S(1)}, f32[2,256]{1,0:T(2,128)}, u32[]{:S(2)}) copy-start(f32[2,256]{1,0:T(2,128)} %copy-done.9) | copy-start | bytes 6148
  348.0 136.1 %copy-start.8 = (f32[2,256]{1,0:T(2,128)S(1)}, f32[2,256]{1,0:T(2,128)}, u32[]{:S(2)}) copy-start(f32[2,256]{1,0:T(2,128)} %copy-done.7) | copy-start | bytes 6148
  384.0 211.2 %all-reduce.6.cloned.1.call-start = ((), (), s32[]{:S(2)}) async-start(), calls=%async_computation.4 | async-start | bytes 2097152 | tf_op jit(solution)/shard_map/psum | solution.py:56
  487.7 1.0 copy-start.3
  490.1 36.5 %copy-start.11 = (f32[2,512]{1,0:T(2,128)S(1)}, f32[2,512]{1,0:T(2,128)}, u32[]{:S(2)}) copy-start(f32[2,512]{1,0:T(2,128)} %get-tuple-element.18) | copy-start | bytes 12292
Sparse Core Ops, SparseCore 0:
  14.7 57.6 all-gather.1
  191.1 103.7 all-reduce.3
  384.2 97.7 reduce-scatter.1
  490.2 105.0 all-reduce.5
where the time goes:
time: 605 us; the launch traced here: 604 us
  waiting for transfers between devices  276 us (46%)
  matrix products  118 us (20%)
  other arithmetic  97.6 us (16%)
  blocking collectives  92 us (15%)
  between operations  14 us (2%)
    psum x1, waiting for transfers between devices, device_step(): glob_stats = lax.psum(part_stats, 'tp')  103 us
    reduce_scatter x1, waiting for transfers between devices, device_step(): dx_loc = lax.psum_scatter(dx_part, 'tp', scatter_dimension=1, tiled=True)  97.6 us
    convert_element_type x1, other arithmetic, device_step(): (jnp.where(is_target, softmax_val - 1.0, softmax_val) * weight[..., None]...  51.1 us
    pmax x1, blocking collectives, device_step(): glob_max = lax.pmax(local_max, 'tp')  43.6 us
    dot_general x1, matrix products, device_step(): jnp.einsum('hsd,vd->hsv', x_all, embed, preferred_element_type=jnp.float32)  41.4 us
    psum x1, waiting for transfers between devices, device_step(): lax.psum((d_w_part, d_scale_part, d_shift_part), 'tp')  40.9 us
    dot_general x1, matrix products, device_step(): jnp.einsum('hsv,vd->hsd', d_logits, embed, preferred_element_type=jnp.flo...  36 us
    dot_general x1, matrix products, device_step(): jnp.einsum('hsv,hsd->vd', d_logits, x_all, preferred_element_type=jnp.flo...  35.3 us
  transfers between devices with their start and end apart: 4, of which 4 were waited for; matrix products, arithmetic and copies ran while one was open for 7% of the time, Pallas kernels for 0%

commit v1 on v0

v1 whole, which is shorter than its diff:
```python
import functools

import jax
import jax.numpy as jnp
from jax import lax
from jax.experimental import pallas as pl
from jax.experimental.pallas import tpu as pltpu
from jax.sharding import PartitionSpec as P

LN_EPS = 1e-5
F32 = jnp.float32
BF16 = jnp.bfloat16
MESH = pl.DeviceIdType.MESH
MASKED = 3.0e38


def dot_nn(a, b):
    return lax.dot_general(a, b, (((1,), (0,)), ((), ())), preferred_element_type=F32)


def dot_nt(a, b):
    return lax.dot_general(a, b, (((1,), (1,)), ((), ())), preferred_element_type=F32)


def norm_rows(val, gain, bias):
    cen = val - jnp.mean(val, axis=-1, keepdims=True)
    var = jnp.mean(cen * cen, axis=-1, keepdims=True)
    return (cen * lax.rsqrt(var + LN_EPS) * gain + bias).astype(BF16)


def kernel(n, chunk, h_ref, w_ref, gain_ref, bias_ref, gcol_ref, e_ref, meta_ref,
           loss_ref, total_ref, dh_ref, de_out, dw_ref, dln_ref,
           h_all, x_all, et, de, dz, meta_all, st_loc, st_rcv, nm_own, nm_all, part, sib, ring,
           at_own, g_own, g_rcv, dwt, sm_own, sm_rcv, xu,
           h_ss, h_rs, meta_ss, meta_rs, st_ss, st_rs, nm_ss, nm_rs, sib_ss, sib_rs, ring_ss, ring_rs,
           g_ss, g_rs, dwt_ss, dwt_rs, sm_ss, sm_rs, de_sem):
    tok, dim = h_ref.shape
    half = tok // 2
    rows = e_ref.shape[0]
    chips = n // 2
    far = chips // 2
    units = n
    me = lax.axis_index('tp')
    zc = me // 2
    kc = lax.rem(me, 2)
    wrap = lambda c: lax.rem(c + 2 * chips, chips)
    right = wrap(zc + 1) * 2 + kc
    left = wrap(zc - 1) * 2 + kc
    other = zc * 2 + 1 - kc
    peer = lambda i: lax.rem(me + i, n)

    def rcopy(src, dst, ss, rs, dev):
        return pltpu.make_async_remote_copy(src_ref=src, dst_ref=dst, send_sem=ss, recv_sem=rs,
                                            device_id={'tp': dev}, device_id_type=MESH)

    barrier = pltpu.get_barrier_semaphore()

    def hello(i, c):
        pl.semaphore_signal(barrier, inc=1, device_id={'tp': peer(i)}, device_id_type=MESH)
        return c
    lax.fori_loop(1, n, hello, 0)
    pl.semaphore_wait(barrier, n - 1)

    def hcopy(kind, chip, part_idx, core):
        owner = chip * 2 + core
        rng = pl.ds(part_idx * half, half)
        dev = (right, left, other)[kind]
        return rcopy(h_all.at[owner, rng], h_all.at[owner, rng], h_ss.at[kind, chip, part_idx],
                     h_rs.at[owner, part_idx], dev)

    def hown(kind, part_idx):
        rng = pl.ds(part_idx * half, half)
        dev = (right, left, other)[kind]
        return rcopy(h_ref.at[rng], h_all.at[me, rng], h_ss.at[kind, zc, part_idx], h_rs.at[me, part_idx], dev)

    for kind, p in ((0, 0), (1, 1), (0, 1), (1, 0), (2, 0), (2, 1)):
        hown(kind, p).start()

    def bcast(src, dst, ss, rs):
        def go(i, c):
            o = peer(i)
            rcopy(src, dst.at[me], ss.at[o], rs.at[me], o).start()
            return c
        lax.fori_loop(1, n, go, 0)

    def wait_recv(dst, ss, rs):
        def go(i, c):
            o = peer(i)
            rcopy(dst.at[o], dst.at[o], ss.at[o], rs.at[o], o).wait_recv()
            return c
        lax.fori_loop(1, n, go, 0)

    def wait_send(dst, ss, rs):
        def go(i, c):
            o = peer(i)
            rcopy(dst.at[o], dst.at[o], ss.at[o], rs.at[o], o).wait_send()
            return c
        lax.fori_loop(1, n, go, 0)

    bcast(meta_ref, meta_all, meta_ss, meta_rs)
    meta_all[me] = meta_ref[...]
    h_all[me] = h_ref[...]

    r_i = lax.broadcasted_iota(jnp.int32, (dim, dim), 0)
    c_i = lax.broadcasted_iota(jnp.int32, (dim, dim), 1)
    eye = jnp.where(r_i == c_i, 1.0, 0.0).astype(BF16)
    for r0 in range(0, rows, chunk):
        et[:, r0:r0 + chunk] = dot_nt(eye, e_ref[r0:r0 + chunk, :]).astype(BF16)
    h_own = h_ref[...]
    at_own[0] = dot_nt(eye, h_own)
    at_own[1] = dot_nt(eye, dot_nn(h_own, w_ref[...]).astype(BF16))

    def chip_block(i, c):
        j = (i + 1) // 2
        lo = wrap(zc - j)
        hi = wrap(zc + j)

        @pl.when(i == 0)
        def _():
            for p in range(2):
                hcopy(2, zc, p, 1 - kc).wait_recv()

        @pl.when((lax.rem(i, 2) == 1) & (j < far))
        def _():
            for p in range(2):
                hcopy(0, lo, p, kc).wait_recv()
                if p == 0:
                    hcopy(0, lo, p, kc).start()
                else:
                    @pl.when(j < far - 1)
                    def _():
                        hcopy(0, lo, p, kc).start()
                hcopy(2, lo, p, kc).start()
                q = 1 - p
                hcopy(1, hi, q, kc).wait_recv()
                if q == 1:
                    hcopy(1, hi, q, kc).start()
                else:
                    @pl.when(j < far - 1)
                    def _():
                        hcopy(1, hi, q, kc).start()
                hcopy(2, hi, q, kc).start()
            for p in range(2):
                hcopy(2, lo, p, 1 - kc).wait_recv()
                hcopy(2, hi, p, 1 - kc).wait_recv()

        @pl.when(j == far)
        def _():
            for p in range(2):
                hcopy(p, lo, p, kc).wait_recv()
                hcopy(2, lo, p, kc).start()
            for p in range(2):
                hcopy(2, lo, p, 1 - kc).wait_recv()

        chip = jnp.where(lax.rem(i, 2) == 1, lo, hi)
        w_two = w_ref[...]
        for q in range(2):
            h_val = h_all[2 * chip + q]
            x_all[0, 2 * chip + q] = norm_rows(h_val.astype(F32), gain_ref[0:1, :], bias_ref[0:1, :])
            a_two = dot_nn(h_val, w_two).astype(BF16).astype(F32)
            x_all[1, 2 * chip + q] = norm_rows(a_two, gain_ref[1:2, :], bias_ref[1:2, :])

        for h in range(2):
            x = x_all[h, pl.ds(2 * chip, 2)].reshape(2 * tok, dim)
            z = dot_nt(e_ref[0:chunk, :], x)
            m = s = None
            for r0 in range(0, rows, chunk):
                z_next = dot_nt(e_ref[r0 + chunk:r0 + 2 * chunk, :], x) if r0 + chunk < rows else None
                z3 = z.reshape(chunk // 8, 8, 2 * tok)
                cm = jnp.max(z3, axis=0)
                if m is None:
                    m = cm
                    s = jnp.sum(jnp.exp(z3 - m[None]), axis=0)
                else:
                    mn = jnp.maximum(m, cm)
                    s = s * jnp.exp(m - mn) + jnp.sum(jnp.exp(z3 - mn[None]), axis=0)
                    m = mn
                z = z_next
            m_all = jnp.max(m, axis=0, keepdims=True)
            s_all = jnp.sum(s * jnp.exp(m - m_all), axis=0, keepdims=True)
            for q in range(2):
                for p in range(2):
                    cut = slice((2 * q + p) * half, (2 * q + p + 1) * half)
                    st_loc[2 * chip + q, 2 * h + p:2 * h + p + 1, :] = m_all[:, cut]
                    st_loc[2 * chip + q, 4 + 2 * h + p:5 + 2 * h + p, :] = s_all[:, cut]
        for q in range(2):
            o = 2 * chip + q

            @pl.when(o != me)
            def _():
                rcopy(st_loc.at[o], st_rcv.at[me], st_ss.at[o], st_rs.at[me], o).start()
        return c
    lax.fori_loop(0, chips, chip_block, 0)

    wait_recv(meta_all, meta_ss, meta_rs)
    counts = jnp.sum(meta_all[:, 4:8, :], axis=0)
    n_tok = []
    for h in range(2):
        two = jnp.sum(counts[2 * h:2 * h + 2, :], axis=1, keepdims=True)
        n_tok += [jnp.sum(two, axis=0, keepdims=True)] * 2
    n_tok = jnp.concatenate(n_tok, axis=0)
    mask = meta_ref[4:8, :]
    weight = mask / n_tok
    st_rcv[me] = st_loc[me]
    wait_recv(st_rcv, st_ss, st_rs)
    st = st_rcv[...]
    st_m, st_s = st[:, 0:4, :], st[:, 4:8, :]
    m_tok = jnp.max(st_m, axis=0)
    s_tok = jnp.sum(st_s * jnp.exp(st_m - m_tok[None]), axis=0)
    lse = m_tok + jnp.log(s_tok)
    lse_w = jnp.where(mask > 0.0, lse - jnp.log(jnp.maximum(weight, 1e-30)), MASKED)
    nm_own[...] = jnp.concatenate([lse_w, weight], axis=0)
    nm_all[me] = nm_own[...]
    bcast(nm_own, nm_all, nm_ss, nm_rs)
    de[...] = jnp.zeros_like(de)
    wait_recv(nm_all, nm_ss, nm_rs)

    sub_i = lax.broadcasted_iota(jnp.int32, (8, half), 0)
    base_row = (me * rows).astype(F32)

    def pick(tile, row):
        return jnp.sum(jnp.where(sub_i == row, tile, 0.0), axis=0, keepdims=True)

    def sib_copy(u):
        return rcopy(part.at[lax.rem(u, 2), 1 - kc], sib.at[u], sib_ss.at[u], sib_rs.at[u], other)

    def ring_copy(u, d):
        return rcopy(sib.at[u, d], ring.at[u, d], ring_ss.at[u, d], ring_rs.at[u, d], (right, left)[d])

    def pass_on(u):
        step = u // 2
        sib_copy(u).wait_recv()
        for d in range(2):
            @pl.when(step > 0)
            def _():
                ring_copy(u - 2, d).wait_recv()
                sib[u, d] = sib[u, d] + part[lax.rem(u, 2), kc, d] + ring[u - 2, d]

            @pl.when(step == 0)
            def _():
                sib[u, d] = sib[u, d] + part[lax.rem(u, 2), kc, d]

            @pl.when(step < chips - 1)
            def _():
                ring_copy(u, d).start()

    def unit(u, c):
        h = 1 - lax.rem(u, 2)
        step = u // 2
        plus = wrap(zc - 1 - step)
        minus = wrap(zc + 1 + step)
        lse_p, w_p, t_p = [], [], []
        for q in range(2):
            for p, chip in ((0, plus), (1, minus)):
                o = 2 * chip + q
                at = 2 * q + p
                xu[at * half:(at + 1) * half, :] = x_all[h, o, p * half:(p + 1) * half, :]
                lse_p.append(pick(nm_all[o], 2 * h + p))
                w_p.append(pick(nm_all[o], 4 + 2 * h + p))
                t_p.append(pick(meta_all[o], 2 * h + p))
        lse_v = jnp.broadcast_to(jnp.concatenate(lse_p, axis=1), (8, 2 * tok))
        w_v = jnp.broadcast_to(jnp.concatenate(w_p, axis=1), (8, 2 * tok))
        row8 = lax.broadcasted_iota(jnp.int32, (8, 2 * tok), 0).astype(F32)
        t_v = jnp.broadcast_to(jnp.concatenate(t_p, axis=1), (8, 2 * tok)) - base_row - row8
        x = xu[...]
        tz = jnp.zeros((8, 2 * tok), F32)
        z = dot_nt(e_ref[0:chunk, :], x)
        for r0 in range(0, rows, chunk):
            z_next = dot_nt(e_ref[r0 + chunk:r0 + 2 * chunk, :], x) if r0 + chunk < rows else None
            for g in range(0, chunk, 16):
                pieces = []
                for b in range(2):
                    z8 = z[g + 8 * b:g + 8 * b + 8, :]
                    hit = t_v == float(r0 + g + 8 * b)
                    tz = tz + jnp.where(hit, z8, 0.0)
                    pieces.append(jnp.exp(z8 - lse_v) - jnp.where(hit, w_v, 0.0))
                dz[r0 + g:r0 + g + 16, :] = jnp.concatenate(pieces, axis=0).astype(BF16)
            de[r0:r0 + chunk, :] += dot_nn(dz[r0:r0 + chunk, :], x)
            z = z_next
        dxt = dot_nn(et[...], dz[...])

        @pl.when(u >= 2)
        def _():
            sib_copy(u - 2).wait_send()
        slot = lax.rem(u, 2)
        for q in range(2):
            for p in range(2):
                cut = slice((2 * q + p) * half, (2 * q + p + 1) * half)
                part[slot, q, p, 0:dim, :] = dxt[:, cut]
                part[slot, q, p, dim:dim + 8, :] = tz[:, cut]
        sib_copy(u).start()

        @pl.when(u >= 1)
        def _():
            pass_on(u - 1)
        return c
    lax.fori_loop(0, units, unit, 0)
    de_copy = pltpu.make_async_copy(de, de_out, de_sem)
    de_copy.start()
    pass_on(units - 1)

    loss_rows = []
    sums = []
    da_all = []
    for h in range(2):
        u = units - 1 - h
        g_col = gcol_ref[:, h:h + 1]
        acc_s = acc_b = None
        da_h = []
        for p in range(2):
            a = at_own[h, :, p * half:(p + 1) * half]
            cen = a - jnp.mean(a, axis=0, keepdims=True)
            rstd = lax.rsqrt(jnp.mean(cen * cen, axis=0, keepdims=True) + LN_EPS)
            xh = cen * rstd
            dx = sib[u, p, 0:dim, :]
            tgt = jnp.sum(sib[u, p, dim:dim + 8, :], axis=0, keepdims=True)
            loss_rows.append((lse[2 * h + p:2 * h + p + 1, :] - tgt) * mask[2 * h + p:2 * h + p + 1, :])
            dy = dx * g_col
            c1 = jnp.mean(dy, axis=0, keepdims=True)
            c2 = jnp.mean(dy * xh, axis=0, keepdims=True)
            da_h.append(rstd * (dy - c1 - xh * c2))
            acc_s = dx * xh if acc_s is None else acc_s + dx * xh
            acc_b = dx if acc_b is None else acc_b + dx
        da_all.append(jnp.concatenate(da_h, axis=1))
        sums.append((jnp.sum(acc_s.T, axis=0, keepdims=True), jnp.sum(acc_b.T, axis=0, keepdims=True)))
    loss = jnp.concatenate(loss_rows, axis=0)
    loss_ref[...] = loss
    frac = loss / n_tok
    loss_row = jnp.concatenate([frac[i:i + 1, :] for i in range(4)], axis=1)
    sm_own[...] = jnp.concatenate([sums[0][0], sums[1][0], sums[0][1], sums[1][1], loss_row,
                                   jnp.zeros((3, dim), F32)], axis=0)
    sm_rcv[me] = sm_own[...]
    bcast(sm_own, sm_rcv, sm_ss, sm_rs)
    d_proj = da_all[1].astype(BF16)
    width = dim // n
    for i in range(n):
        g_own[i] = d_proj[i * width:(i + 1) * width, :]
    g_rcv[me] = g_own[me]

    def g_send(i, c):
        o = peer(i)
        rcopy(g_own.at[o], g_rcv.at[me], g_ss.at[o], g_rs.at[me], o).start()
        return c
    lax.fori_loop(1, n, g_send, 0)
    dht = da_all[0] + dot_nn(w_ref[...], d_proj)
    dh_ref[...] = dht.T.astype(BF16)

    wait_recv(g_rcv, g_ss, g_rs)
    dw_slice = jnp.zeros((width, dim), F32)
    for o in range(n):
        dw_slice = dw_slice + dot_nn(g_rcv[o], h_all[o])
    dwt[me] = dw_slice

    def dw_send(i, c):
        o = peer(i)
        rcopy(dwt.at[me], dwt.at[me], dwt_ss.at[o], dwt_rs.at[me], o).start()
        return c
    lax.fori_loop(1, n, dw_send, 0)

    wait_recv(sm_rcv, sm_ss, sm_rs)
    sm = jnp.sum(sm_rcv[...], axis=0)
    dln_ref[...] = sm[0:4, :]
    total_ref[...] = jnp.broadcast_to(jnp.sum(sm[4:5, :], axis=1, keepdims=True), total_ref.shape)
    wait_recv(dwt, dwt_ss, dwt_rs)
    dw_ref[...] = dwt[...].reshape(dim, dim).T

    for ref, ss, rs in ((meta_all, meta_ss, meta_rs), (st_rcv, st_ss, st_rs), (nm_all, nm_ss, nm_rs),
                        (g_rcv, g_ss, g_rs), (dwt, dwt_ss, dwt_rs), (sm_rcv, sm_ss, sm_rs)):
        wait_send(ref, ss, rs)
    for kind in range(3):
        for p in range(2):
            hown(kind, p).wait_send()

    def h_done(j, c):
        lo = wrap(zc - j)
        hi = wrap(zc + j)
        hcopy(0, lo, 0, kc).wait_send()
        hcopy(1, hi, 1, kc).wait_send()

        @pl.when(j < far - 1)
        def _():
            hcopy(0, lo, 1, kc).wait_send()
            hcopy(1, hi, 0, kc).wait_send()
        for p in range(2):
            hcopy(2, lo, p, kc).wait_send()
            hcopy(2, hi, p, kc).wait_send()
        return c
    lax.fori_loop(1, far, h_done, 0)
    for p in range(2):
        hcopy(2, wrap(zc + far), p, kc).wait_send()
    for u in (units - 2, units - 1):
        sib_copy(u).wait_send()

    def ring_done(u, c):
        for d in range(2):
            ring_copy(u, d).wait_send()
        return c
    lax.fori_loop(0, units - 2, ring_done, 0)
    de_copy.wait()


def pick_chunk(rows):
    best = 128
    for c in range(128, min(rows, 640) + 1, 128):
        if rows % c == 0:
            best = c
    return best


def solution(mesh):
    n = mesh.shape['tp']
    tok_spec = P(('dp', 'tp'), None)
    row_spec = P(None, ('dp', 'tp'))

    def device_step(hidden, w_two, ln_scale, ln_shift, embed, targets, loss_mask):
        tok, dim = hidden.shape
        half = tok // 2
        rows = embed.shape[0]
        width = dim // n
        meta = jnp.concatenate([targets.reshape(4, half), loss_mask.reshape(4, half)], axis=0).astype(F32)
        vmem = pl.BlockSpec(memory_space=pltpu.VMEM)
        dma = pltpu.SemaphoreType.DMA
        outs = pl.pallas_call(
            functools.partial(kernel, n, pick_chunk(rows)),
            name='two_head_step',
            out_shape=(jax.ShapeDtypeStruct((4, half), F32),
                       jax.ShapeDtypeStruct((1, 128), F32),
                       jax.ShapeDtypeStruct((tok, dim), BF16),
                       jax.ShapeDtypeStruct((rows, dim), F32),
                       jax.ShapeDtypeStruct((dim, dim), F32),
                       jax.ShapeDtypeStruct((4, dim), F32)),
            in_specs=[vmem] * 7,
            out_specs=(vmem, vmem, vmem, pl.BlockSpec(memory_space=pl.ANY), vmem, vmem),
            scratch_shapes=[
                pltpu.VMEM((n, tok, dim), BF16),
                pltpu.VMEM((2, n, tok, dim), BF16),
                pltpu.VMEM((dim, rows), BF16),
                pltpu.VMEM((rows, dim), F32),
                pltpu.VMEM((rows, 2 * tok), BF16),
                pltpu.VMEM((n, 8, half), F32),
                pltpu.VMEM((n, 8, half), F32),
                pltpu.VMEM((n, 8, half), F32),
                pltpu.VMEM((8, half), F32),
                pltpu.VMEM((n, 8, half), F32),
                pltpu.VMEM((2, 2, 2, dim + 8, half), F32),
                pltpu.VMEM((n, 2, dim + 8, half), F32),
                pltpu.VMEM((n, 2, dim + 8, half), F32),
                pltpu.VMEM((2, dim, tok), F32),
                pltpu.VMEM((n, width, tok), BF16),
                pltpu.VMEM((n, width, tok), BF16),
                pltpu.VMEM((n, width, dim), F32),
                pltpu.VMEM((8, dim), F32),
                pltpu.VMEM((n, 8, dim), F32),
                pltpu.VMEM((2 * tok, dim), BF16),
                dma((3, n // 2, 2)), dma((n, 2)),
                dma((n,)), dma((n,)), dma((n,)), dma((n,)), dma((n,)), dma((n,)),
                dma((n,)), dma((n,)), dma((n, 2)), dma((n, 2)),
                dma((n,)), dma((n,)), dma((n,)), dma((n,)), dma((n,)), dma((n,)),
                dma,
            ],
            compiler_params=pltpu.CompilerParams(collective_id=0, has_side_effects=True,
                                                 vmem_limit_bytes=67043328),
        )(hidden, w_two, ln_scale, ln_shift, ln_scale.T, embed, meta)
        loss, total, d_hidden, d_embed, d_w_two, d_ln = outs
        return (loss.reshape(2, tok), total[0, :1], d_hidden, d_embed, d_w_two, d_ln[0:2], d_ln[2:4])

    return jax.shard_map(device_step, mesh=mesh,
                         in_specs=(tok_spec, P(), P(), P(), P('tp', None), row_spec, row_spec),
                         out_specs=(row_spec, P('dp'), tok_spec, tok_spec, P('dp', None), P('dp', None), P('dp', None)),
                         check_vma=False)
```

time: 605 us -> 235 us (0.39)
  waiting for transfers between devices: 276 us -> 0 us
  Pallas kernels: 0 us -> 217 us
  matrix products: 118 us -> 0 us
  other arithmetic: 97.6 us -> 0.6 us
  blocking collectives: 92 us -> 0 us
  between operations: 14 us -> 2.41 us
  local copies, waits for them, and re-layouts: 5.9 us -> 14.7 us
    pallas_call x0 -> x1, Pallas kernels: none -> 217 us  [device_step(): pl.pallas_call(functools.partial(kernel, n, pick_chunk(rows)), name='two_...]
    psum x2 -> x0, waiting for transfers between devices: 144 us -> none  [the longest x1 103 us: device_step(): glob_stats = lax.psum(part_stats, 'tp')]
    dot_general x6 -> x0, matrix products: 118 us -> none  [the longest x1 41.4 us: device_step(): jnp.einsum('hsd,vd->hsv', x_all, embed, preferred_element_type=jnp.float32)]
    reduce_scatter x1 -> x0, waiting for transfers between devices: 97.6 us -> none  [device_step(): dx_loc = lax.psum_scatter(dx_part, 'tp', scatter_dimension=1, tiled=True)]
    convert_element_type x2 -> x1, other arithmetic: 53.1 us -> 0.6 us  [device_step(): jnp.concatenate([targets.reshape(4, half), loss_mask.reshape(4, half)], a...]
    pmax x1 -> x0, blocking collectives: 43.6 us -> none  [device_step(): glob_max = lax.pmax(local_max, 'tp')]
    reduce_sum x7 -> x0, other arithmetic: 41.4 us -> none  [the longest x1 32.7 us: device_step(): jnp.sum(exp_loc, axis=-1) * jnp.exp(local_max - glob_max)]
    all_gather x1 -> x0, waiting for transfers between devices: 34 us -> none  [device_step(): x_all = lax.all_gather(x_loc, 'tp', axis=1, tiled=True)]
  transfers between devices with their start and end apart: 4 -> 0, of which waited for: 4 -> 0; matrix products, arithmetic and copies ran while one was open for 7% -> 0% of each run, Pallas kernels for 0% -> 0%
where the time goes in v1:
time: 235 us; the launch traced here: 234 us
  Pallas kernels  217 us (92%)
  local copies, waits for them, and re-layouts  14.7 us (6%)
  between operations  2.41 us (1%)
    pallas_call x1, Pallas kernels, device_step(): pl.pallas_call(functools.partial(kernel, n, pick_chunk(rows)), name='two_...  217 us
    unnamed x6, local copies, waits for them, and re-layouts  10.7 us

profile of v1, /device:TPU:21, one launch (start us, length us, event | category | flops | bytes accessed | tf_op | source)
XLA Modules:
  0.0 234.3 jit_solution(17451389186981436924)
XLA Ops:
  0.6 0.7 reshape.23
  1.3 0.7 reshape.24
  2.0 0.6 add_convert_fusion.meta_ref
  2.6 1.5 copy.14
  4.2 216.6 %two_head_step.1 = (f32[4,128]{1,0:T(4,128)}, f32[1,128]{1,0:T(1,128)}, bf16[256,512]{1,0:T(8,128)(2,1)}, f32[3200,512]{1,0:T(8,128)}, f32[512,512]{1,0:T(8,128)}, /*index=5*/f32[4,512]{1,0:T(4,128)}) custom-call(bf16[256,512]{1,0:T(8,128)(2,1)} %h_ref.1, bf16[512,512]{1,0:T(8,128)(2,1)} %w_ref.1, f32[2,512]{1,0:T(2,128)} %gain_ref.1, f32[2,512]{1,0:T(2,128)} %bias_ref.1, ...), custom_call_target="tpu_custom_call" | custom-call | tf_op jit(solution)/shard_map/two_head_step/pallas_call | solution.py:423
  220.8 1.3 reshape.25
  222.1 1.4 fusion
  224.1 1.7 copy.20
  225.7 0.0 copy-start
  225.7 6.5 %copy.21 = f32[3200,512]{1,0:T(8,128)} copy(f32[3200,512]{1,0:T(8,128)} %get-tuple-element.31) | data formatting | bytes 13107200
  232.2 0.0 copy-done
  232.2 1.0 copy.22
Async XLA Ops:
  225.7 6.5 %copy-start = (f32[512,512]{1,0:T(8,128)S(1)}, f32[512,512]{1,0:T(8,128)}, u32[]{:S(2)}) copy-start(f32[512,512]{1,0:T(8,128)} %get-tuple-element.32) | copy-start | bytes 3145732

commit v2 on v0

v2 whole, which is shorter than its diff:
```python
import functools

import jax
import jax.numpy as jnp
from jax import lax
from jax.experimental import pallas as pl
from jax.experimental.pallas import tpu as pltpu
from jax.sharding import PartitionSpec as P

LN_EPS = 1e-5
F32 = jnp.float32
BF16 = jnp.bfloat16
MESH = pl.DeviceIdType.MESH
MASKED = 3.0e38
GROUP = 64


def dot_nn(a, b):
    return lax.dot_general(a, b, (((1,), (0,)), ((), ())), preferred_element_type=F32)


def dot_nt(a, b):
    return lax.dot_general(a, b, (((1,), (1,)), ((), ())), preferred_element_type=F32)


def norm_rows(val, gain, bias):
    cen = val - jnp.mean(val, axis=-1, keepdims=True)
    var = jnp.mean(cen * cen, axis=-1, keepdims=True)
    return (cen * lax.rsqrt(var + LN_EPS) * gain + bias).astype(BF16)


def kernel(n, chunk, h_ref, w_ref, gain_ref, bias_ref, e_ref, tgt_ref, mask_ref,
           loss_ref, total_ref, dh_ref, de_out, dw_ref, dsc_ref, dsh_ref,
           h_all, x_all, et, de, dz, meta_own, meta_all, st_loc, st_rcv, nm_own, nm_all, lse_own, gcol,
           part, sib, ring, at_own, g_own, g_rcv, dwt, sm_own, sm_rcv, xu,
           h_ss, h_rs, meta_ss, meta_rs, st_ss, st_rs, nm_ss, nm_rs, sib_ss, sib_rs, ring_ss, ring_rs,
           g_ss, g_rs, dwt_ss, dwt_rs, sm_ss, sm_rs, de_sem):
    tok, dim = h_ref.shape
    half = tok // 2
    rows = e_ref.shape[0]
    chips = n // 2
    far = chips // 2
    units = n
    width = dim // n
    cols = dim // half
    me = lax.axis_index('tp')
    zc = me // 2
    kc = lax.rem(me, 2)
    wrap = lambda c: lax.rem(c + 2 * chips, chips)
    right = wrap(zc + 1) * 2 + kc
    left = wrap(zc - 1) * 2 + kc
    other = zc * 2 + 1 - kc
    peer = lambda i: lax.rem(me + i, n)

    def rcopy(src, dst, ss, rs, dev):
        return pltpu.make_async_remote_copy(src_ref=src, dst_ref=dst, send_sem=ss, recv_sem=rs,
                                            device_id={'tp': dev}, device_id_type=MESH)

    def each(lo, hi, fn):
        def go(i, c):
            fn(i)
            return c
        lax.fori_loop(lo, hi, go, 0)

    tgt_f = tgt_ref[...].astype(F32)
    mask_f = mask_ref[...].astype(F32)
    meta_own[...] = jnp.concatenate([v[h:h + 1, p * half:(p + 1) * half]
                                     for v in (tgt_f, mask_f) for h in range(2) for p in range(2)], axis=0)

    barrier = pltpu.get_barrier_semaphore()
    each(1, n, lambda i: pl.semaphore_signal(barrier, inc=1, device_id={'tp': peer(i)}, device_id_type=MESH))
    pl.semaphore_wait(barrier, n - 1)

    def gcopy(g, kind, chip, p, core, src=None):
        buf, ss, rs = g
        owner = chip * 2 + core
        cut = buf.shape[1] // 2
        rng = pl.ds(p * cut, cut)
        at = buf.at[owner, rng]
        return rcopy(at if src is None else src.at[rng], at, ss.at[kind, chip, p], rs.at[owner, p],
                     (right, left, other)[kind])

    own_order = ((0, 0), (1, 1), (2, 0), (2, 1), (0, 1), (1, 0))

    def gather_own(g, src=None):
        for kind, p in own_order:
            gcopy(g, kind, zc, p, kc, src).start()

    def gather_step(g, j):
        lo = wrap(zc - j)
        hi = wrap(zc + j)

        @pl.when(j < far)
        def _():
            for p in range(2):
                gcopy(g, 0, lo, p, kc).wait_recv()
                if p == 0:
                    gcopy(g, 0, lo, p, kc).start()
                else:
                    @pl.when(j < far - 1)
                    def _():
                        gcopy(g, 0, lo, p, kc).start()
                gcopy(g, 2, lo, p, kc).start()
                q = 1 - p
                gcopy(g, 1, hi, q, kc).wait_recv()
                if q == 1:
                    gcopy(g, 1, hi, q, kc).start()
                else:
                    @pl.when(j < far - 1)
                    def _():
                        gcopy(g, 1, hi, q, kc).start()
                gcopy(g, 2, hi, q, kc).start()

        @pl.when(j == far)
        def _():
            for p in range(2):
                gcopy(g, p, lo, p, kc).wait_recv()
                gcopy(g, 2, lo, p, kc).start()

    def gather_other(g, chip):
        for p in range(2):
            gcopy(g, 2, chip, p, 1 - kc).wait_recv()

    def gather_done(g, src=None):
        for kind, p in own_order:
            gcopy(g, kind, zc, p, kc, src).wait_send()

        def sent(j):
            lo = wrap(zc - j)
            hi = wrap(zc + j)
            gcopy(g, 0, lo, 0, kc).wait_send()
            gcopy(g, 1, hi, 1, kc).wait_send()

            @pl.when(j < far - 1)
            def _():
                gcopy(g, 0, lo, 1, kc).wait_send()
                gcopy(g, 1, hi, 0, kc).wait_send()
            for p in range(2):
                gcopy(g, 2, lo, p, kc).wait_send()
                gcopy(g, 2, hi, p, kc).wait_send()
        each(1, far, sent)
        for p in range(2):
            gcopy(g, 2, wrap(zc + far), p, kc).wait_send()

    h_net = (h_all, h_ss, h_rs)
    dw_net = (dwt, dwt_ss, dwt_rs)
    gather_own(h_net, h_ref)

    def bcast(src, dst, ss, rs):
        each(1, n, lambda i: rcopy(src, dst.at[me], ss.at[peer(i)], rs.at[me], peer(i)).start())

    def wait_recv(dst, ss, rs):
        each(1, n, lambda i: rcopy(dst.at[peer(i)], dst.at[peer(i)], ss.at[peer(i)], rs.at[peer(i)],
                                   peer(i)).wait_recv())

    def wait_send(dst, ss, rs):
        each(1, n, lambda i: rcopy(dst.at[peer(i)], dst.at[peer(i)], ss.at[peer(i)], rs.at[peer(i)],
                                   peer(i)).wait_send())

    bcast(meta_own, meta_all, meta_ss, meta_rs)
    meta_all[me] = meta_own[...]
    h_all[me] = h_ref[...]

    r_i = lax.broadcasted_iota(jnp.int32, (dim, dim), 0)
    c_i = lax.broadcasted_iota(jnp.int32, (dim, dim), 1)
    eye = jnp.where(r_i == c_i, 1.0, 0.0).astype(BF16)
    for r0 in range(0, rows, chunk):
        et[:, r0:r0 + chunk] = dot_nt(eye, e_ref[r0:r0 + chunk, :]).astype(BF16)
    h_own = h_ref[...]
    at_own[0] = dot_nt(eye, h_own)
    at_own[1] = dot_nt(eye, dot_nn(h_own, w_ref[...]).astype(BF16))
    for h in range(2):
        gcol[h] = jnp.broadcast_to(gain_ref[h:h + 1, :], (half, dim)).T

    def normalize(chip):
        w_two = w_ref[...]
        x_two = []
        for q in range(2):
            a_two = dot_nn(h_all[2 * chip + q], w_two).astype(BF16).astype(F32)
            x_two.append(norm_rows(a_two, gain_ref[1:2, :], bias_ref[1:2, :]))
        for q in range(2):
            x_all[1, 2 * chip + q] = x_two[q]
            x_all[0, 2 * chip + q] = norm_rows(h_all[2 * chip + q].astype(F32), gain_ref[0:1, :], bias_ref[0:1, :])
        return jnp.concatenate(x_two, axis=0)

    def stored(h, chip):
        return x_all[h, pl.ds(2 * chip, 2)].reshape(2 * tok, dim)

    def first_pass(jobs):
        stream = [(k, r0) for k in range(len(jobs)) for r0 in range(0, rows, chunk)]
        logits = lambda k, r0: dot_nt(e_ref[r0:r0 + chunk, :], jobs[k][2])
        z = logits(*stream[0])
        m = s = None
        for at, (k, r0) in enumerate(stream):
            z_next = logits(*stream[at + 1]) if at + 1 < len(stream) else None
            for g in range(0, chunk, GROUP):
                z3 = z[g:g + GROUP, :].reshape(GROUP // 8, 8, 2 * tok)
                cm = jnp.max(z3, axis=0)
                if r0 + g == 0:
                    m = cm
                    s = jnp.sum(jnp.exp(z3 - m[None]), axis=0)
                else:
                    mn = jnp.maximum(m, cm)
                    s = s * jnp.exp(m - mn) + jnp.sum(jnp.exp(z3 - mn[None]), axis=0)
                    m = mn
            if r0 + chunk == rows:
                h, chip, _ = jobs[k]
                m_all = jnp.max(m, axis=0, keepdims=True)
                s_all = jnp.sum(s * jnp.exp(m - m_all), axis=0, keepdims=True)
                for q in range(2):
                    for p in range(2):
                        cut = slice((2 * q + p) * half, (2 * q + p + 1) * half)
                        st_loc[h, 2 * chip + q, p:p + 1, :] = m_all[:, cut]
                        st_loc[h, 2 * chip + q, 2 + p:3 + p, :] = s_all[:, cut]
            z = z_next
        for h, chip, _ in jobs:
            for q in range(2):
                o = 2 * chip + q

                @pl.when(o != me)
                def _():
                    rcopy(st_loc.at[h, o], st_rcv.at[h, me], st_ss.at[h, o], st_rs.at[h, me], o).start()

    def head_count(h):
        two = jnp.sum(jnp.sum(meta_all[:, 4 + 2 * h:6 + 2 * h, :], axis=0), axis=1, keepdims=True)
        return jnp.sum(two, axis=0, keepdims=True)

    def combine(h):
        st_rcv[h, me] = st_loc[h, me]
        wait_recv(st_rcv.at[h], st_ss.at[h], st_rs.at[h])
        mask = meta_own[4 + 2 * h:6 + 2 * h, :]
        weight = mask / head_count(h)
        st = st_rcv[h]
        st_m, st_s = st[:, 0:2, :], st[:, 2:4, :]
        m_tok = jnp.max(st_m, axis=0)
        s_tok = jnp.sum(st_s * jnp.exp(st_m - m_tok[None]), axis=0)
        lse = m_tok + jnp.log(s_tok)
        lse_w = jnp.where(mask > 0.0, lse - jnp.log(jnp.maximum(weight, 1e-30)), MASKED)
        lse_own[h, 0:2, :] = lse
        nm_own[h] = jnp.concatenate([lse_w, weight, jnp.zeros((4, half), F32)], axis=0)
        nm_all[h, me] = nm_own[h]
        bcast(nm_own.at[h], nm_all.at[h], nm_ss.at[h], nm_rs.at[h])

    def stage(k):
        lo = wrap(zc - k)
        hi = wrap(zc + k)
        one = jnp.where(k == 0, zc, wrap(zc + far))

        @pl.when(k == 0)
        def _():
            gather_other(h_net, zc)

        @pl.when((k > 0) & (k <= far))
        def _():
            gather_step(h_net, k)

        @pl.when((k > 0) & (k < far))
        def _():
            gather_other(h_net, lo)
            gather_other(h_net, hi)
            first_pass([(1, lo, normalize(lo)), (1, hi, normalize(hi))])

        @pl.when(k == far)
        def _():
            gather_other(h_net, one)

        @pl.when((k == 0) | (k == far))
        def _():
            first_pass([(1, one, normalize(one))])

        @pl.when((k > 0) & (k <= far) & (k != far - 1))
        def _():
            back = jnp.minimum(k, far - 1)
            near = (wrap(zc - back), wrap(zc + back))
            first_pass([(0, c, stored(0, c)) for c in near])

        @pl.when(k == far + 1)
        def _():
            wait_recv(meta_all, meta_ss, meta_rs)
            combine(1)

        @pl.when((k == 0) | (k == far + 1))
        def _():
            first_pass([(0, one, stored(0, one))])
    each(0, far + 2, stage)
    de[...] = jnp.zeros_like(de)
    wait_recv(nm_all.at[1], nm_ss.at[1], nm_rs.at[1])

    sub_i = lax.broadcasted_iota(jnp.int32, (8, half), 0)
    base_row = (me * rows).astype(F32)

    def pick(tile, row):
        return jnp.sum(jnp.where(sub_i == row, tile, 0.0), axis=0, keepdims=True)

    def sib_copy(u):
        return rcopy(part.at[lax.rem(u, 2), 1 - kc], sib.at[u], sib_ss.at[u], sib_rs.at[u], other)

    cuts = ((0, dim // 2), (dim // 2, dim // 2 + 8))

    def ring_copy(u, d, ab):
        rng = pl.ds(*cuts[ab])
        return rcopy(sib.at[u, d, rng], ring.at[u, d, rng], ring_ss.at[u, d, ab], ring_rs.at[u, d, ab],
                     (right, left)[d])

    def pass_on(u, ab):
        step = lax.rem(u, chips)
        rng = pl.ds(*cuts[ab])
        slot = lax.rem(u, 2)
        if ab == 0:
            sib_copy(u).wait_recv()
        for d in range(2):
            @pl.when(step > 0)
            def _():
                ring_copy(u - 1, d, ab).wait_recv()
                sib[u, d, rng] = sib[u, d, rng] + part[slot, kc, d, rng] + ring[u - 1, d, rng]

            @pl.when(step == 0)
            def _():
                sib[u, d, rng] = sib[u, d, rng] + part[slot, kc, d, rng]

            @pl.when(step < chips - 1)
            def _():
                ring_copy(u, d, ab).start()

    def finish(h, u):
        acc_s = acc_b = None
        da_h, frac = [], []
        n_tok = head_count(h)
        for p in range(2):
            a = at_own[h, :, p * half:(p + 1) * half]
            cen = a - jnp.mean(a, axis=0, keepdims=True)
            rstd = lax.rsqrt(jnp.mean(cen * cen, axis=0, keepdims=True) + LN_EPS)
            xh = cen * rstd
            dx = sib[u, p, 0:dim, :]
            tgt = jnp.sum(sib[u, p, dim:dim + 8, :], axis=0, keepdims=True)
            row = (lse_own[h, p:p + 1, :] - tgt) * meta_own[4 + 2 * h + p:5 + 2 * h + p, :]
            loss_ref[h:h + 1, p * half:(p + 1) * half] = row
            frac.append(row / n_tok)
            dy = dx * gcol[h]
            c1 = jnp.mean(dy, axis=0, keepdims=True)
            c2 = jnp.mean(dy * xh, axis=0, keepdims=True)
            da_h.append(rstd * (dy - c1 - xh * c2))
            acc_s = dx * xh if acc_s is None else acc_s + dx * xh
            acc_b = dx if acc_b is None else acc_b + dx
        d_sc = jnp.sum(acc_s.T, axis=0, keepdims=True)
        d_sh = jnp.sum(acc_b.T, axis=0, keepdims=True)
        lines = [v[:, j * half:(j + 1) * half] for v in (d_sc, d_sh) for j in range(cols)] + frac
        sm_own[h] = jnp.concatenate(lines + [jnp.zeros((16 - len(lines), half), F32)], axis=0)
        sm_rcv[h, me] = sm_own[h]
        bcast(sm_own.at[h], sm_rcv.at[h], sm_ss.at[h], sm_rs.at[h])
        return jnp.concatenate(da_h, axis=1)

    def events(u):
        @pl.when(u == 1)
        def _():
            combine(0)

        @pl.when(u == 5)
        def _():
            wait_recv(nm_all.at[0], nm_ss.at[0], nm_rs.at[0])

        @pl.when(u == chips)
        def _():
            d_proj = finish(1, chips - 1).astype(BF16)
            for i in range(n):
                g_own[i] = d_proj[i * width:(i + 1) * width, :]
            g_rcv[me] = g_own[me]
            each(1, n, lambda i: rcopy(g_own.at[peer(i)], g_rcv.at[me], g_ss.at[peer(i)], g_rs.at[me],
                                       peer(i)).start())
            at_own[1] = dot_nn(w_ref[...], d_proj)

        @pl.when(u == chips + 2)
        def _():
            wait_recv(g_rcv, g_ss, g_rs)
            dw_slice = jnp.zeros((width, dim), F32)
            for o in range(n):
                dw_slice = dw_slice + dot_nn(g_rcv[o], h_all[o])
            dwt[me] = dw_slice
            gather_own(dw_net)

        @pl.when((u > chips + 2) & (u <= chips + 2 + far))
        def _():
            gather_step(dw_net, u - chips - 2)

        @pl.when(u == units - 1)
        def _():
            each(0, chips, lambda c: gather_other(dw_net, c))
            dw_ref[...] = dwt[...].reshape(dim, dim).T

    def unit(u):
        h = 1 - u // chips
        step = lax.rem(u, chips)
        plus = wrap(zc - 1 - step)
        minus = wrap(zc + 1 + step)
        lse_p, w_p, t_p = [], [], []
        for q in range(2):
            for p, chip in ((0, plus), (1, minus)):
                o = 2 * chip + q
                at = 2 * q + p
                xu[at * half:(at + 1) * half, :] = x_all[h, o, p * half:(p + 1) * half, :]
                tile = nm_all[h, o]
                lse_p.append(tile[p:p + 1, :])
                w_p.append(tile[2 + p:3 + p, :])
                t_p.append(pick(meta_all[o], 2 * h + p))
        lse_v = jnp.broadcast_to(jnp.concatenate(lse_p, axis=1), (8, 2 * tok))
        w_v = jnp.broadcast_to(jnp.concatenate(w_p, axis=1), (8, 2 * tok))
        row8 = lax.broadcasted_iota(jnp.int32, (8, 2 * tok), 0).astype(F32)
        t_v = jnp.broadcast_to(jnp.concatenate(t_p, axis=1), (8, 2 * tok)) - base_row - row8
        x = xu[...]
        tz = jnp.zeros((8, 2 * tok), F32)
        z = dot_nt(e_ref[0:chunk, :], x)
        mid = max(rows - 2 * chunk, 0)
        for r0 in range(0, rows, chunk):
            z_next = dot_nt(e_ref[r0 + chunk:r0 + 2 * chunk, :], x) if r0 + chunk < rows else None
            for g in range(0, chunk, 16):
                pieces = []
                for b in range(2):
                    z8 = z[g + 8 * b:g + 8 * b + 8, :]
                    hit = t_v == float(r0 + g + 8 * b)
                    tz = tz + jnp.where(hit, z8, 0.0)
                    pieces.append(jnp.exp(z8 - lse_v) - jnp.where(hit, w_v, 0.0))
                dz[r0 + g:r0 + g + 16, :] = jnp.concatenate(pieces, axis=0).astype(BF16)
            de[r0:r0 + chunk, :] += dot_nn(dz[r0:r0 + chunk, :], x)
            z = z_next
            if r0 == mid:
                @pl.when(u >= 1)
                def _():
                    pass_on(u - 1, 0)
        dxt = dot_nn(et[...], dz[...])

        @pl.when(u >= 2)
        def _():
            sib_copy(u - 2).wait_send()
        slot = lax.rem(u, 2)
        for q in range(2):
            for p in range(2):
                cut = slice((2 * q + p) * half, (2 * q + p + 1) * half)
                part[slot, q, p, 0:dim, :] = dxt[:, cut]
                part[slot, q, p, dim:dim + 8, :] = tz[:, cut]
        sib_copy(u).start()

        @pl.when(u >= 1)
        def _():
            pass_on(u - 1, 1)
        events(u)
    each(0, units, unit)
    de_copy = pltpu.make_async_copy(de, de_out, de_sem)
    de_copy.start()
    last = units - 1
    pass_on(last, 0)
    pass_on(last, 1)
    d_a1 = finish(0, last)
    dh_ref[...] = (d_a1 + at_own[1]).T.astype(BF16)

    wait_send(meta_all, meta_ss, meta_rs)
    for h in range(2):
        wait_send(st_rcv.at[h], st_ss.at[h], st_rs.at[h])
        wait_send(nm_all.at[h], nm_ss.at[h], nm_rs.at[h])
        wait_send(sm_rcv.at[h], sm_ss.at[h], sm_rs.at[h])
    wait_send(g_rcv, g_ss, g_rs)
    gather_done(h_net, h_ref)
    gather_done(dw_net)
    for u in (units - 2, units - 1):
        sib_copy(u).wait_send()

    def ring_done(u):
        @pl.when(lax.rem(u, chips) < chips - 1)
        def _():
            for d in range(2):
                for ab in range(2):
                    ring_copy(u, d, ab).wait_send()
    each(0, units, ring_done)

    for h in (1, 0):
        wait_recv(sm_rcv.at[h], sm_ss.at[h], sm_rs.at[h])
    total = 0.0
    for h in range(2):
        sm = jnp.sum(sm_rcv[h], axis=0)
        for j in range(cols):
            dsc_ref[h:h + 1, j * half:(j + 1) * half] = sm[j:j + 1, :]
            dsh_ref[h:h + 1, j * half:(j + 1) * half] = sm[cols + j:cols + j + 1, :]
        total = total + jnp.sum(sm[2 * cols:2 * cols + 2, :])
    total_ref[0] = total
    de_copy.wait()


def pick_chunk(rows):
    best = 128
    for c in range(128, min(rows, 640) + 1, 128):
        if rows % c == 0:
            best = c
    return best


def solution(mesh):
    n = mesh.shape['tp']
    tok_spec = P(('dp', 'tp'), None)
    row_spec = P(None, ('dp', 'tp'))

    def device_step(hidden, w_two, ln_scale, ln_shift, embed, targets, loss_mask):
        tok, dim = hidden.shape
        half = tok // 2
        rows = embed.shape[0]
        width = dim // n
        vmem = pl.BlockSpec(memory_space=pltpu.VMEM)
        dma = pltpu.SemaphoreType.DMA
        return pl.pallas_call(
            functools.partial(kernel, n, pick_chunk(rows)),
            name='two_head_step',
            out_shape=(jax.ShapeDtypeStruct((2, tok), F32),
                       jax.ShapeDtypeStruct((1,), F32),
                       jax.ShapeDtypeStruct((tok, dim), BF16),
                       jax.ShapeDtypeStruct((rows, dim), F32),
                       jax.ShapeDtypeStruct((dim, dim), F32),
                       jax.ShapeDtypeStruct((2, dim), F32),
                       jax.ShapeDtypeStruct((2, dim), F32)),
            in_specs=[vmem] * 7,
            out_specs=(vmem, pl.BlockSpec(memory_space=pltpu.SMEM), vmem, pl.BlockSpec(memory_space=pl.ANY),
                       vmem, vmem, vmem),
            scratch_shapes=[
                pltpu.VMEM((n, tok, dim), BF16),
                pltpu.VMEM((2, n, tok, dim), BF16),
                pltpu.VMEM((dim, rows), BF16),
                pltpu.VMEM((rows, dim), F32),
                pltpu.VMEM((rows, 2 * tok), BF16),
                pltpu.VMEM((8, half), F32),
                pltpu.VMEM((n, 8, half), F32),
                pltpu.VMEM((2, n, 8, half), F32),
                pltpu.VMEM((2, n, 8, half), F32),
                pltpu.VMEM((2, 8, half), F32),
                pltpu.VMEM((2, n, 8, half), F32),
                pltpu.VMEM((2, 8, half), F32),
                pltpu.VMEM((2, dim, half), F32),
                pltpu.VMEM((2, 2, 2, dim + 8, half), F32),
                pltpu.VMEM((n, 2, dim + 8, half), F32),
                pltpu.VMEM((n, 2, dim + 8, half), F32),
                pltpu.VMEM((2, dim, tok), F32),
                pltpu.VMEM((n, width, tok), BF16),
                pltpu.VMEM((n, width, tok), BF16),
                pltpu.VMEM((n, width, dim), F32),
                pltpu.VMEM((2, 16, half), F32),
                pltpu.VMEM((2, n, 16, half), F32),
                pltpu.VMEM((2 * tok, dim), BF16),
                dma((3, n // 2, 2)), dma((n, 2)),
                dma((n,)), dma((n,)), dma((2, n)), dma((2, n)), dma((2, n)), dma((2, n)),
                dma((n,)), dma((n,)), dma((n, 2, 2)), dma((n, 2, 2)),
                dma((n,)), dma((n,)), dma((3, n // 2, 2)), dma((n, 2)), dma((2, n)), dma((2, n)),
                dma,
            ],
            compiler_params=pltpu.CompilerParams(collective_id=0, has_side_effects=True,
                                                 vmem_limit_bytes=67043328),
        )(hidden, w_two, ln_scale, ln_shift, embed, targets, loss_mask)

    return jax.shard_map(device_step, mesh=mesh,
                         in_specs=(tok_spec, P(), P(), P(), P('tp', None), row_spec, row_spec),
                         out_specs=(row_spec, P('dp'), tok_spec, tok_spec, P('dp', None), P('dp', None), P('dp', None)),
                         check_vma=False)
```

time: 605 us -> 203 us (0.34)
  waiting for transfers between devices: 276 us -> 0 us
  Pallas kernels: 0 us -> 189 us
  matrix products: 118 us -> 0 us
  other arithmetic: 97.6 us -> 0 us
  blocking collectives: 92 us -> 0 us
  between operations: 14 us -> 2.4 us
    pallas_call x0 -> x1, Pallas kernels: none -> 189 us  [device_step(): pl.pallas_call(functools.partial(kernel, n, pick_chunk(rows)), name='two_...]
    psum x2 -> x0, waiting for transfers between devices: 144 us -> none  [the longest x1 103 us: device_step(): glob_stats = lax.psum(part_stats, 'tp')]
    dot_general x6 -> x0, matrix products: 118 us -> none  [the longest x1 41.4 us: device_step(): jnp.einsum('hsd,vd->hsv', x_all, embed, preferred_element_type=jnp.float32)]
    reduce_scatter x1 -> x0, waiting for transfers between devices: 97.6 us -> none  [device_step(): dx_loc = lax.psum_scatter(dx_part, 'tp', scatter_dimension=1, tiled=True)]
    convert_element_type x2 -> x0, other arithmetic: 53.1 us -> none  [the longest x1 51.1 us: device_step(): (jnp.where(is_target, softmax_val - 1.0, softmax_val) * weight[..., None]...]
    pmax x1 -> x0, blocking collectives: 43.6 us -> none  [device_step(): glob_max = lax.pmax(local_max, 'tp')]
    reduce_sum x7 -> x0, other arithmetic: 41.4 us -> none  [the longest x1 32.7 us: device_step(): jnp.sum(exp_loc, axis=-1) * jnp.exp(local_max - glob_max)]
    all_gather x1 -> x0, waiting for transfers between devices: 34 us -> none  [device_step(): x_all = lax.all_gather(x_loc, 'tp', axis=1, tiled=True)]
  transfers between devices with their start and end apart: 4 -> 0, of which waited for: 4 -> 0; matrix products, arithmetic and copies ran while one was open for 7% -> 0% of each run, Pallas kernels for 0% -> 0%
where the time goes in v2:
time: 203 us
  Pallas kernels  189 us (93%)
  local copies, waits for them, and re-layouts  11.6 us (6%)
  between operations  2.4 us (1%)
    pallas_call x1, Pallas kernels, device_step(): pl.pallas_call(functools.partial(kernel, n, pick_chunk(rows)), name='two_...  189 us
    unnamed x12, local copies, waits for them, and re-layouts  11.6 us

profile of v2, /device:TPU:21, one launch (start us, length us, event | category | flops | bytes accessed | tf_op | source)
XLA Modules:
  0.0 202.5 jit_solution(13509213277645759815)
XLA Ops:
  0.6 188.5 %two_head_step.1 = (f32[2,256]{1,0:T(2,128)}, f32[1]{0:T(128)}, bf16[256,512]{1,0:T(8,128)(2,1)}, f32[3200,512]{1,0:T(8,128)}, f32[512,512]{1,0:T(8,128)}, /*index=5*/f32[2,512]{1,0:T(2,128)}, f32[2,512]{1,0:T(2,128)}) custom-call(bf16[256,512]{1,0:T(8,128)(2,1)} %h_ref.1, bf16[512,512]{1,0:T(8,128)(2,1)} %w_ref.1, f32[2,512]{1,0:T(2,128)} %gain_ref.1, ...), custom_call_target="tpu_custom_call" | custom-call | tf_op jit(solution)/shard_map/two_head_step/pallas_call | solution.py:507
  189.2 1.3 copy.21
  191.1 1.7 copy.23
  192.7 0.0 copy-start
  192.7 0.0 copy-start.2
  192.7 0.0 copy-start.1
  192.7 6.5 %copy.24 = f32[3200,512]{1,0:T(8,128)} copy(f32[3200,512]{1,0:T(8,128)} %get-tuple-element.17) | data formatting | bytes 13107200
  199.2 0.0 copy-done
  199.2 1.0 copy.25
  200.2 0.0 copy-done.2
  200.2 0.6 copy.26
  200.8 0.0 copy-done.1
  200.8 0.6 copy.27
Async XLA Ops:
  192.7 6.5 %copy-start = (f32[512,512]{1,0:T(8,128)S(1)}, f32[512,512]{1,0:T(8,128)}, u32[]{:S(2)}) copy-start(f32[512,512]{1,0:T(8,128)} %get-tuple-element.18) | copy-start | bytes 3145732
  192.7 7.5 %copy-start.2 = (f32[2,512]{1,0:T(2,128)S(1)}, f32[2,512]{1,0:T(2,128)}, u32[]{:S(2)}) copy-start(f32[2,512]{1,0:T(2,128)} %get-tuple-element.19) | copy-start | bytes 12292
  192.7 8.1 %copy-start.1 = (f32[2,512]{1,0:T(2,128)S(1)}, f32[2,512]{1,0:T(2,128)}, u32[]{:S(2)}) copy-start(f32[2,512]{1,0:T(2,128)} %get-tuple-element.20) | copy-start | bytes 12292

commit v3 on v2

--- a/solution.py
+++ b/solution.py
@@ -492,6 +492,27 @@
     return best
 
 
+def flush_kernel(*refs):
+    count = len(refs) // 2
+
+    @pl.when(pl.program_id(0) == 0)
+    def _():
+        refs[count][0] = refs[0][0]
+        for i in range(2, count):
+            refs[count + i][...] = refs[i][...]
+    refs[count + 1][...] = refs[1][...]
+
+
+def flush(total, d_embed, *small):
+    rows, dim = d_embed.shape
+    block = pick_chunk(rows)
+    big = pl.BlockSpec((block, dim), lambda i: (i, 0))
+    specs = [pl.BlockSpec(memory_space=pltpu.SMEM), big] + [pl.BlockSpec(v.shape, lambda i: (0, 0)) for v in small]
+    outs = [total, d_embed, *small]
+    return pl.pallas_call(flush_kernel, name='flush', grid=(rows // block,), in_specs=specs, out_specs=specs,
+                          out_shape=[jax.ShapeDtypeStruct(v.shape, v.dtype) for v in outs])(*outs)
+
+
 def solution(mesh):
     n = mesh.shape['tp']
     tok_spec = P(('dp', 'tp'), None)
@@ -504,7 +525,7 @@
         width = dim // n
         vmem = pl.BlockSpec(memory_space=pltpu.VMEM)
         dma = pltpu.SemaphoreType.DMA
-        return pl.pallas_call(
+        loss, total, d_hidden, d_embed, d_w_two, d_sc, d_sh, *_ = pl.pallas_call(
             functools.partial(kernel, n, pick_chunk(rows)),
             name='two_head_step',
             out_shape=(jax.ShapeDtypeStruct((2, tok), F32),
@@ -550,6 +571,8 @@
             compiler_params=pltpu.CompilerParams(collective_id=0, has_side_effects=True,
                                                  vmem_limit_bytes=67043328),
         )(hidden, w_two, ln_scale, ln_shift, embed, targets, loss_mask)
+        total, d_embed, loss, d_hidden, d_w_two, d_sc, d_sh = flush(total, d_embed, loss, d_hidden, d_w_two, d_sc, d_sh)
+        return loss, total, d_hidden, d_embed, d_w_two, d_sc, d_sh
 
     return jax.shard_map(device_step, mesh=mesh,
                          in_specs=(tok_spec, P(), P(), P(), P('tp', None), row_spec, row_spec),

time: 203 us -> 198 us (0.975)
  local copies, waits for them, and re-layouts: 11.6 us -> 0 us
  Pallas kernels: 189 us -> 197 us
    unnamed x12 -> x0, local copies, waits for them, and re-layouts: 11.6 us -> none
    pallas_call x0 -> x1, Pallas kernels: none -> 8.92 us  [flush(): pl.pallas_call(flush_kernel, name='flush', grid=(rows // block,), in_spec...]
where the time goes in v3:
time: 198 us
  Pallas kernels  197 us (99%)
    pallas_call x1, Pallas kernels, device_step(): pl.pallas_call(functools.partial(kernel, n, pick_chunk(rows)), name='two_...  189 us
    pallas_call x1, Pallas kernels, flush(): pl.pallas_call(flush_kernel, name='flush', grid=(rows // block,), in_spec...  8.92 us

profile of v3, /device:TPU:21, one launch (start us, length us, event | category | flops | bytes accessed | tf_op | source)
XLA Modules:
  0.0 198.3 jit_solution(4892332911476135892)
XLA Ops:
  0.6 188.5 %two_head_step.1 = (f32[2,256]{1,0:T(2,128)}, f32[1]{0:T(128)}, bf16[256,512]{1,0:T(8,128)(2,1)}, f32[3200,512]{1,0:T(8,128)}, f32[512,512]{1,0:T(8,128)}, /*index=5*/f32[2,512]{1,0:T(2,128)}, f32[2,512]{1,0:T(2,128)}) custom-call(bf16[256,512]{1,0:T(8,128)(2,1)} %h_ref.1, bf16[512,512]{1,0:T(8,128)(2,1)} %w_ref.1, f32[2,512]{1,0:T(2,128)} %gain_ref.1, ...), custom_call_target="tpu_custom_call" | custom-call | tf_op jit(solution)/shard_map/two_head_step/pallas_call | solution.py:528
  189.2 8.9 %flush.1 = (f32[1]{0:T(128)}, f32[3200,512]{1,0:T(8,128)}, f32[2,256]{1,0:T(2,128)}, bf16[256,512]{1,0:T(8,128)(2,1)}, f32[512,512]{1,0:T(8,128)}, /*index=5*/f32[2,512]{1,0:T(2,128)}, f32[2,512]{1,0:T(2,128)}) custom-call(f32[1]{0:T(128)} %get-tuple-element.21.refs_0_, f32[3200,512]{1,0:T(8,128)} %get-tuple-element.22.refs_1_, ...), custom_call_target="tpu_custom_call" | custom-call | tf_op jit(solution)/shard_map/flush/pallas_call | solution.py:512
